TPU v7x, 32 devices: a whole 2x2x4 slice. The times are simulated.
32 devices in a mesh: region: 8 (over z, x), member: 4 (over y, core).
Axes of the slice: x: 2, y: 2, z: 4, core: 2. Of those that a mesh axis runs over, the one named last changes fastest.
Arguments:
- ensemble: bfloat16 [40, 131072], P('member', 'region'), may hold values from -6 to 6
- obs_value: float32 [1024, 128], P(('region', 'member')), may hold values from -8 to 8
- obs_var: float32 [1024, 128], P(('region', 'member')), may hold values from 0.1 to 1
- obs_point: int32 [1024, 128], P(('region', 'member')), may hold values from 0 to 16383
- owned_blocks: int32 [1024], P('region'), may hold values from 0 to 1023, each once
- infl_mean: float32 [1024], replicated, may hold values from 0.6 to 1.6
- infl_var: float32 [1024], replicated, may hold values from 0.0001 to 0.1
Outputs:
- inflated: bfloat16 [40, 131072], P('member', 'region')
- infl_post: float32 [1024], P(('region', 'member'))
Inputs may be any that keep to these rules, and one draw needn't show every extreme that they name: `obs_point`: index among the 16384 points of the observation's region; the observation belongs to the block of that point's slot. `owned_blocks`: every block id appears exactly once.
All inputs are finite; a program needn't handle non-finite values.
Results may differ from a plain program's by a relative error of at most 0.001.
Values sent between devices are 32-bit elements; how exact they have to be, the bound alone decides.
A program may use at most 64 MiB of HBM per device.

v0:
```python
import jax
import jax.numpy as jnp
from jax import lax
from jax.sharding import PartitionSpec as P


def posterior(sums, prior_mean, prior_var):
    innov_sum = sums[0]
    spread_sum = sums[1]
    error_sum = sums[2]
    spread_spread = sums[3]
    spread_error = sums[4]
    error_error = sums[5]
    weight_var = (
        2.0 * prior_mean * prior_mean * (1.0 + spread_spread)
        + 4.0 * prior_mean * spread_error
        + 2.0 * error_error
    )
    value = (prior_mean * weight_var + prior_var * spread_sum * (innov_sum - error_sum)) / (
        weight_var + prior_var * spread_sum * spread_sum
    )
    return jnp.maximum(value, 1.0)


def bin_slots(innovation, spread, errors, slot_of, slots):
    count = innovation.shape[0]
    width = min(count, 2048)
    while count % width != 0:
        width = width // 2
    blocks = count // width
    inno = innovation.reshape(blocks, width)
    sprd = spread.reshape(blocks, width)
    errs = errors.reshape(blocks, width)
    columns = jnp.stack([inno * inno, sprd, errs, sprd * sprd, sprd * errs, errs * errs], 1)
    labels = slot_of.reshape(blocks, width)
    slot_ids = jnp.arange(slots, dtype=jnp.int32)

    def one_block(carry, pair):
        block_cols, block_labels = pair
        onehot = (block_labels[:, None] == slot_ids[None, :]).astype(jnp.float32)
        return (
            carry
            + jnp.dot(
                block_cols,
                onehot,
                precision=lax.Precision.HIGHEST,
                preferred_element_type=jnp.float32,
            ),
            None,
        )

    total, unused = lax.scan(one_block, jnp.zeros((6, slots), jnp.float32), (columns, labels))
    return total


def body(ensemble, obs_value, obs_var, obs_point, owned_blocks, infl_mean, infl_var):
    members = ensemble.shape[0] * lax.axis_size("member")
    wide = ensemble.astype(jnp.float32)
    local_total = jnp.sum(wide, 0)
    local_square = jnp.sum(wide * wide, 0)
    own_points = obs_point.reshape(-1)
    point_total, point_square = lax.psum((local_total, local_square), "member")
    point_mean = point_total / members
    at_square = point_square[own_points]
    at_mean = point_mean[own_points]
    spread = (at_square - members * at_mean * at_mean) / (members - 1)
    innovation = obs_value.reshape(-1) - at_mean
    errors = obs_var.reshape(-1)
    slots = owned_blocks.shape[0]
    span = point_mean.shape[0] // slots
    slot_of = own_points // span
    slot_sums = bin_slots(innovation, spread, errors, slot_of, slots)
    num_blocks = infl_mean.shape[0]
    share = num_blocks // lax.axis_size(("region", "member"))
    first = lax.axis_index(("region", "member")) * share
    placed_sums = jnp.zeros((6, num_blocks), jnp.float32).at[:, owned_blocks].set(slot_sums)
    totals = lax.psum(placed_sums, ("region", "member"))
    lambda_all = posterior(totals, infl_mean, infl_var)
    lambda_mine = lax.dynamic_slice_in_dim(lambda_all, first, share)
    lambda_owned = lambda_all[owned_blocks]
    factor = jnp.sqrt(lambda_owned)[None, :, None]
    mean_slots = point_mean.reshape(1, slots, -1)
    shaped = wide.reshape(wide.shape[0], slots, -1)
    inflated = (
        (mean_slots + factor * (shaped - mean_slots)).astype(jnp.bfloat16).reshape(ensemble.shape)
    )
    return (inflated, lambda_mine)


def solution(mesh):
    placed = (
        P("member", "region"),
        P(("region", "member"), None),
        P(("region", "member"), None),
        P(("region", "member"), None),
        P("region"),
        P(),
        P(),
    )
    return jax.shard_map(
        body,
        mesh=mesh,
        in_specs=placed,
        out_specs=(P("member", "region"), P(("region", "member"))),
        check_vma=False,
    )
```

profile of v0, /device:TPU:0, one launch (start us, length us, event | category | flops | bytes accessed | tf_op | source)
XLA Modules:
  0.0 151.9 jit_solution(3200294530436090924)
XLA Ops:
  7.2 0.0 all-reduce.3.cloned.1.call-start
  7.2 2.2 %fusion.6 = (f32[16384]{0:T(1024)}, f32[16384]{0:T(1024)}) fusion(bf16[10,16384]{1,0:T(8,128)(2,1)} %param.9), kind=kLoop, calls=%fused_computation.15 | loop fusion | flops 622592 | bytes 458752 | tf_op jit(solution)/shard_map/reduce_sum | solution.py:60
  9.4 0.0 all-reduce.3.cloned.1.call-update
  9.4 0.7 copy-done.3
  10.2 0.0 copy-start.7
  10.2 0.6 copy-done.7
  10.9 34.6 %all-reduce.3.cloned.1.call-done = (f32[16384]{0:T(1024)}, f32[16384]{0:T(1024)}) async-done(((f32[16384]{0:T(1024)}, f32[16384]{0:T(1024)}), (f32[16384]{0:T(1024)}, f32[16384]{0:T(1024)})) %all-reduce.3.cloned.1.call-update) | async-done | bytes 131088 | tf_op jit(solution)/shard_map/psum | solution.py:62
  45.5 0.8 broadcast_multiply_fusion
  46.4 23.0 %gather_fusion = f32[4096]{0:T(1024)S(1)} fusion(f32[16384]{0:T(1024)S(1)} %broadcast_multiply_fusion, s32[4096]{0:T(1024)S(1)} %broadcast_clamp_fusion), kind=kCustom, calls=%fused_computation | custom fusion | bytes 49152 | tf_op jit(solution)/shard_map/gather | solution.py:65
  69.4 0.0 copy-start.4
  69.4 23.0 %gather_fusion.1 = f32[4096]{0:T(1024)S(1)} fusion(f32[16384]{0:T(1024)S(1)} %copy-done, s32[4096]{0:T(1024)S(1)} %broadcast_clamp_fusion), kind=kCustom, calls=%fused_computation.1 | custom fusion | bytes 49152 | tf_op jit(solution)/shard_map/gather | solution.py:64
  92.5 0.1 fusion.20
  92.6 0.2 stack.2
  92.7 1.2 while.11
  92.8 0.6 convolution_add_fusion.2
  93.4 0.6 convolution_add_fusion.2
  94.0 0.1 copy.10
  94.1 1.0 scatter_custom_fusion
  95.1 45.8 %psum.23 = f32[6,1024]{0,1:T(8,128)S(1)} all-reduce(f32[6,1024]{0,1:T(8,128)S(1)} %scatter_custom_fusion), channel_id=1, replica_groups=mesh['region'=8,'member'=4] {'region','member'}, use_global_device_ids=true, to_apply=%region_7.8 | all-reduce | flops 6144 | bytes 49152 | tf_op jit(solution)/shard_map/psum | solution.py:77
  141.0 1.4 slice_reduce_fusion.1
  142.5 1.0 gather_fusion.2
  143.5 0.1 broadcast_bitcast_fusion
  143.5 1.0 fusion.9
  144.5 0.6 dynamic_slice.11
  (24 shorter events, 0.2 us)
Async XLA Ops:
  7.2 38.3 %all-reduce.3.cloned.1.call-start = ((), (), s32[]{:S(2)}) async-start(), calls=%async_computation | async-start | bytes 262144 | tf_op jit(solution)/shard_map/psum | solution.py:62
  9.4 0.7 copy-start.3
  10.2 0.7 copy-start.7
  46.3 23.0 %copy-start = (f32[16384]{0:T(1024)S(1)}, f32[16384]{0:T(1024)}, u32[]{:S(2)}) copy-start(f32[16384]{0:T(1024)} %get-tuple-element.63) | copy-start | bytes 196612
  69.4 23.1 %copy-start.2 = (f32[32,128]{1,0:T(8,128)S(1)}, f32[32,128]{1,0:T(8,128)}, u32[]{:S(2)}) copy-start(f32[32,128]{1,0:T(8,128)} %param.11) | copy-start | bytes 49156
  69.4 23.1 %copy-start.4 = (f32[32,128]{1,0:T(8,128)S(1)}, f32[32,128]{1,0:T(8,128)}, u32[]{:S(2)}) copy-start(f32[32,128]{1,0:T(8,128)} %param.10) | copy-start | bytes 49156
  140.9 1.5 copy-start.5
  141.0 1.5 copy-start.6
  142.4 1.1 copy-start.1
Sparse Core Ops, SparseCore 0:
  10.9 34.5 all-reduce.2
where the time goes:
time: 152 us
  local copies, waits for them, and re-layouts  50.4 us (33%)
  blocking collectives  45.8 us (30%)
  waiting for transfers between devices  34.6 us (23%)
  between operations  14.3 us (9%)
  other arithmetic  5.59 us (4%)
    psum x1, blocking collectives, body(): totals = lax.psum(placed_sums, ('region', 'member'))  45.8 us
    psum x1, waiting for transfers between devices, body(): point_total, point_square = lax.psum((local_total, local_square), 'member')  34.6 us
    gather x1, local copies, waits for them, and re-layouts, body(): at_mean = point_mean[own_points]  23 us
    gather x1, local copies, waits for them, and re-layouts, body(): at_square = point_square[own_points]  23 us
  transfers between devices with their start and end apart: 1, of which 1 were waited for; matrix products, arithmetic and copies ran while one was open for 0% of the time, Pallas kernels for 0%

commit v1 on v0

v1 whole, which is shorter than its diff:
```python
import functools

import jax
import jax.numpy as jnp
from jax import lax
from jax.experimental import pallas as pl
from jax.experimental.pallas import tpu as pltpu
from jax.sharding import PartitionSpec as P

LANES = 128
MESH = pl.DeviceIdType.MESH
F32 = jnp.float32
BF16 = jnp.bfloat16
NT = (((1,), (1,)), ((), ()))


def split(value, parts):
    terms = []
    for _ in range(parts):
        term = value.astype(BF16).astype(F32)
        terms.append(term)
        value = value - term
    return terms


def to_row(table):
    slots = table.shape[0]
    eye = lax.broadcasted_iota(jnp.int32, (slots, slots), 0) == lax.broadcasted_iota(
        jnp.int32, (slots, slots), 1
    )
    column = jnp.sum(table, axis=1, keepdims=True)
    return jnp.sum(jnp.where(eye, column, 0.0), axis=0, keepdims=True)


def scatter(value_ref, var_ref, point_ref, acc, half):
    rows = point_ref.shape[0]
    step = 8
    planes = 10
    low_ids = lax.broadcasted_iota(jnp.int32, (half, LANES), 0)
    col_ids = lax.broadcasted_iota(jnp.int32, (2 * LANES, LANES), 0)

    def chunk(first):
        point = point_ref[pl.ds(first, step), :]
        slot = point >> 7
        upper = (slot >= half).astype(jnp.int32)
        low = slot - half * upper
        col = (point & (LANES - 1)) + LANES * upper
        y = split(value_ref[pl.ds(first, step), :], 2)
        exact = y[0] + y[1]
        v = var_ref[pl.ds(first, step), :]
        terms = [jnp.ones_like(v)] + y + split(exact * exact, 3) + split(v, 2) + split(v * v, 2)
        left, right = [], []
        for r in range(step):
            hot = (low_ids == low[r : r + 1, :]).astype(F32).astype(BF16)
            blocks = []
            for term in terms:
                wide = jnp.broadcast_to(term[r : r + 1, :], (16, LANES)).astype(BF16)
                blocks.append(hot * jnp.concatenate([wide] * (half // 16), 0))
            left.append(jnp.concatenate(blocks, 0))
            right.append((col_ids == col[r : r + 1, :]).astype(F32).astype(BF16))
        return lax.dot_general(
            jnp.concatenate(left, 1), jnp.concatenate(right, 1), NT, preferred_element_type=F32
        )

    acc[...] = chunk(0)

    @pl.loop(1, rows // step)
    def _(i):
        acc[...] += chunk(pl.multiple_of(i * step, step))

    def plane(i, j):
        part = acc[pl.ds(i * half, half), :]
        for other in range(i + 1, j):
            part = part + acc[pl.ds(other * half, half), :]
        return jnp.concatenate([part[:, :LANES], part[:, LANES:]], 0)

    return plane


def kernel(
    n_region, n_member, members,
    ens_hbm, value_hbm, var_hbm, point_hbm, owned_hbm, pmean_hbm, pvar_hbm,
    out_ref, post_ref,
    ens, value, var, point, owned, pmean, pvar,
    part, rs_recv, gathered, stats, factor, acc, place, place_recv,
    in_sem, rs_send, rs_got, ag_send, ag_got, st_send, st_got, pl_send, pl_got,
):
    region = lax.axis_index("region")
    me = lax.axis_index("member")
    slots = owned.shape[1]
    own = slots // n_member
    half = slots // 2

    barrier = pltpu.get_barrier_semaphore()
    for i in range(1, n_member):
        pl.semaphore_signal(
            barrier, inc=1, device_id={"member": lax.rem(me + i, n_member)}, device_id_type=MESH
        )
    for i in range(1, n_region):
        pl.semaphore_signal(
            barrier, inc=1, device_id={"region": lax.rem(region + i, n_region)}, device_id_type=MESH
        )
    pairs = (
        (ens_hbm, ens), (value_hbm, value), (var_hbm, var), (point_hbm, point),
        (owned_hbm, owned), (pmean_hbm, pmean), (pvar_hbm, pvar),
    )
    loads = [pltpu.make_async_copy(s, d, in_sem.at[i]) for i, (s, d) in enumerate(pairs)]
    for load in loads:
        load.start()

    loads[0].wait()

    @pl.loop(0, n_member)
    def _(k):
        @pl.loop(0, own, unroll=8)
        def _(r):
            start = pl.multiple_of((k * own + r) * LANES, LANES)
            wide = ens[:, pl.ds(start, LANES)].astype(F32)
            part[k, pl.ds(r, 1), :] = jnp.sum(wide, 0, keepdims=True)
            part[k, pl.ds(own + r, 1), :] = jnp.sum(wide * wide, 0, keepdims=True)

    pl.semaphore_wait(barrier, n_member + n_region - 2)
    rs = []
    for i in range(1, n_member):
        peer = lax.rem(me + i, n_member)
        copy = pltpu.make_async_remote_copy(
            part.at[peer], rs_recv.at[i], rs_send.at[i], rs_got.at[i],
            device_id={"member": peer}, device_id_type=MESH,
        )
        copy.start()
        rs.append(copy)

    for load in loads[1:]:
        load.wait()
    plane = scatter(value, var, point, acc, half)

    for copy in rs:
        copy.wait_recv()
    both = part[me]
    for i in range(1, n_member):
        both = both + rs_recv[i]
    mean_own = both[:own] / members
    gathered[me, :own, :] = mean_own
    gathered[me, own:, :] = (both[own:] - members * mean_own * mean_own) / (members - 1)
    ag = []
    for i in range(1, n_member):
        copy = pltpu.make_async_remote_copy(
            gathered.at[me], gathered.at[me], ag_send.at[i], ag_got.at[i],
            device_id={"member": lax.rem(me + i, n_member)}, device_id_type=MESH,
        )
        copy.start()
        ag.append(copy)

    block = owned[...]
    groups = pmean.shape[0]
    lane_hot = (
        lax.broadcasted_iota(jnp.int32, (LANES, slots), 0) == (block & (LANES - 1))
    ).astype(F32).astype(BF16)
    table = jnp.concatenate(split(pmean[...], 3) + split(pvar[...], 3), 0).astype(BF16)
    picked = jnp.dot(table, lane_hot, preferred_element_type=F32)
    in_group = lax.broadcasted_iota(jnp.int32, (groups, slots), 0) == (block >> 7)

    def pick(first):
        total = picked[first * groups : (first + 1) * groups]
        for i in (1, 2):
            total = total + picked[(first + i) * groups : (first + i + 1) * groups]
        return jnp.sum(jnp.where(in_group, total, 0.0), 0, keepdims=True)

    prior_mean, prior_var = pick(0), pick(3)
    count, y_sum, y_square, v_sum, v_square = (
        plane(0, 1), plane(1, 3), plane(3, 6), plane(6, 8), plane(8, 10)
    )
    error_sum = to_row(v_sum)
    error_error = to_row(v_square)

    for copy in ag:
        copy.wait_recv()
    mean = jnp.concatenate([gathered[k, :own, :] for k in range(n_member)], 0)
    spread = jnp.concatenate([gathered[k, own:, :] for k in range(n_member)], 0)
    seen = count * spread
    mine = jnp.concatenate(
        [
            to_row(y_square + mean * (count * mean - 2.0 * y_sum)),
            to_row(seen),
            error_sum,
            to_row(seen * spread),
            to_row(v_sum * spread),
            error_error,
            jnp.zeros((2, slots), F32),
        ],
        0,
    )
    stats[0] = mine
    st = []
    for i in range(1, n_member):
        copy = pltpu.make_async_remote_copy(
            stats.at[0], stats.at[i], st_send.at[i], st_got.at[i],
            device_id={"member": lax.rem(me + i, n_member)}, device_id_type=MESH,
        )
        copy.start()
        st.append(copy)
    for copy in st:
        copy.wait_recv()
    total = mine
    for i in range(1, n_member):
        total = total + stats[i]
    sd, sp, so = total[0:1], total[1:2], total[2:3]
    spp, spo, soo = total[3:4], total[4:5], total[5:6]
    weight = 2.0 * prior_mean * prior_mean * (1.0 + spp) + 4.0 * prior_mean * spo + 2.0 * soo
    post = jnp.maximum(
        (prior_mean * weight + prior_var * sp * (sd - so)) / (weight + prior_var * sp * sp), 1.0
    )

    share = groups * LANES // (n_region * n_member)
    holder = block // share
    to_me = lax.rem(holder, n_member) == me
    rows = max(8, n_region)
    target = lax.broadcasted_iota(jnp.int32, (rows, slots), 0) == jnp.where(
        to_me, holder // n_member, -1
    )
    spots = (
        lax.broadcasted_iota(jnp.int32, (LANES, slots), 0) == lax.rem(block, share)
    ).astype(F32).astype(BF16)
    sent = jnp.concatenate([jnp.where(target, term, 0.0) for term in split(post, 3)], 0)
    placed = lax.dot_general(sent.astype(BF16), spots, NT, preferred_element_type=F32)
    placed = placed[:rows] + placed[rows : 2 * rows] + placed[2 * rows :]
    for r in range(n_region):
        place[r] = placed[r : r + 1]
    out_copies = []
    for i in range(1, n_region):
        there = lax.rem(region + i, n_region)
        copy = pltpu.make_async_remote_copy(
            place.at[there], place_recv.at[i], pl_send.at[i], pl_got.at[i],
            device_id={"region": there}, device_id_type=MESH,
        )
        copy.start()
        out_copies.append(copy)

    eye = lax.broadcasted_iota(jnp.int32, (slots, slots), 0) == lax.broadcasted_iota(
        jnp.int32, (slots, slots), 1
    )
    column = jnp.sum(jnp.where(eye, post, 0.0), axis=1, keepdims=True)
    factor[...] = jnp.broadcast_to(jnp.sqrt(column), factor.shape)

    @pl.loop(0, n_member)
    def _(k):
        @pl.loop(0, own, unroll=8)
        def _(r):
            slot = k * own + r
            start = pl.multiple_of(slot * LANES, LANES)
            wide = ens[:, pl.ds(start, LANES)].astype(F32)
            at = gathered[k, pl.ds(r, 1), :]
            out_ref[:, pl.ds(start, LANES)] = (
                at + factor[pl.ds(slot, 1), :] * (wide - at)
            ).astype(BF16)

    for copy in out_copies:
        copy.wait_recv()
    result = place[region]
    for i in range(1, n_region):
        result = result + place_recv[i]
    post_ref[...] = result[:, :share]
    for copy in rs + ag + st + out_copies:
        copy.wait_send()


def body(n_region, n_member, ensemble, obs_value, obs_var, obs_point, owned, infl_mean, infl_var):
    members = ensemble.shape[0] * n_member
    slots = owned.shape[0]
    own = slots // n_member
    blocks = infl_mean.shape[0]
    share = blocks // (n_region * n_member)
    owned = owned.reshape(1, slots)
    infl_mean = infl_mean.reshape(-1, LANES)
    infl_var = infl_var.reshape(-1, LANES)
    operands = (ensemble, obs_value, obs_var, obs_point, owned, infl_mean, infl_var)
    dma = pltpu.SemaphoreType.DMA
    inflated, post = pl.pallas_call(
        functools.partial(kernel, n_region, n_member, members),
        out_shape=(
            jax.ShapeDtypeStruct(ensemble.shape, BF16),
            jax.ShapeDtypeStruct((1, share), F32),
        ),
        in_specs=[pl.BlockSpec(memory_space=pltpu.HBM)] * len(operands),
        out_specs=(
            pl.BlockSpec(memory_space=pltpu.VMEM),
            pl.BlockSpec(memory_space=pltpu.VMEM),
        ),
        scratch_shapes=[pltpu.VMEM(a.shape, a.dtype) for a in operands]
        + [
            pltpu.VMEM((n_member, 2 * own, LANES), F32),
            pltpu.VMEM((n_member, 2 * own, LANES), F32),
            pltpu.VMEM((n_member, 2 * own, LANES), F32),
            pltpu.VMEM((n_member, 8, slots), F32),
            pltpu.VMEM((slots, LANES), F32),
            pltpu.VMEM((10 * (slots // 2), 2 * LANES), F32),
            pltpu.VMEM((n_region, 1, LANES), F32),
            pltpu.VMEM((n_region, 1, LANES), F32),
            dma((len(operands),)),
            dma((n_member,)), dma((n_member,)),
            dma((n_member,)), dma((n_member,)),
            dma((n_member,)), dma((n_member,)),
            dma((n_region,)), dma((n_region,)),
        ],
        compiler_params=pltpu.CompilerParams(collective_id=0, has_side_effects=True),
    )(*operands)
    return inflated, post.reshape(share)


def solution(mesh):
    placed = (
        P("member", "region"),
        P(("region", "member"), None),
        P(("region", "member"), None),
        P(("region", "member"), None),
        P("region"),
        P(),
        P(),
    )
    return jax.shard_map(
        functools.partial(body, mesh.shape["region"], mesh.shape["member"]),
        mesh=mesh,
        in_specs=placed,
        out_specs=(P("member", "region"), P(("region", "member"))),
        check_vma=False,
    )
```

time: 152 us -> 23.1 us (0.15)
  local copies, waits for them, and re-layouts: 50.4 us -> 2.38 us
  blocking collectives: 45.8 us -> 0 us
  waiting for transfers between devices: 34.6 us -> 0 us
  Pallas kernels: 0 us -> 19.9 us
  between operations: 14.3 us -> 0.65 us
  other arithmetic: 5.59 us -> 0 us
    gather x3 -> x0, local copies, waits for them, and re-layouts: 47 us -> none  [the longest x1 23 us: body(): at_mean = point_mean[own_points]]
    psum x1 -> x0, blocking collectives: 45.8 us -> none  [body(): totals = lax.psum(placed_sums, ('region', 'member'))]
    psum x1 -> x0, waiting for transfers between devices: 34.6 us -> none  [body(): point_total, point_square = lax.psum((local_total, local_square), 'member')]
    pallas_call x0 -> x1, Pallas kernels: none -> 19.9 us  [body(): pl.pallas_call(functools.partial(kernel, n_region, n_member, members), ou...]
    reduce_sum x1 -> x0, other arithmetic: 2.17 us -> none  [body(): local_square = jnp.sum(wide * wide, 0)]
  transfers between devices with their start and end apart: 1 -> 0, of which waited for: 1 -> 0; matrix products, arithmetic and copies ran while one was open for 0% -> 0% of each run, Pallas kernels for 0% -> 0%
where the time goes in v1:
time: 23.1 us; the launch traced here: 22.9 us
  Pallas kernels  19.9 us (86%)
  local copies, waits for them, and re-layouts  2.38 us (10%)
  between operations  0.65 us (3%)
    pallas_call x1, Pallas kernels, body(): pl.pallas_call(functools.partial(kernel, n_region, n_member, members), ou...  19.9 us
    unnamed x4, local copies, waits for them, and re-layouts  2.38 us

profile of v1, /device:TPU:0, one launch (start us, length us, event | category | flops | bytes accessed | tf_op | source)
XLA Modules:
  0.0 22.9 jit_solution(16228040691127658431)
XLA Ops:
  0.6 19.9 %shard_map.86 = (bf16[10,16384]{1,0:T(8,128)(2,1)}, f32[1,32]{1,0:T(1,128)}) custom-call(bf16[10,16384]{1,0:T(8,128)(2,1)} %ens_hbm.1, f32[32,128]{1,0:T(8,128)} %value_hbm.1, f32[32,128]{1,0:T(8,128)} %var_hbm.1, s32[32,128]{1,0:T(8,128)} %point_hbm.1, s32[1,128]{1,0:T(1,128)} %bitcast.6, f32[8,128]{1,0:T(8,128)} %bitcast.4, f32[8,128]{1,0:T(8,128)} %bitcast.5), custom_call_target="tpu_custom_call" | custom-call | tf_op jit(solution)/shard_map/pallas_call | solution.py:278
  20.6 0.0 copy-start
  20.6 1.9 %copy.11 = bf16[10,16384]{1,0:T(8,128)(2,1)} copy(bf16[10,16384]{1,0:T(8,128)(2,1)} %get-tuple-element.8) | data formatting | bytes 655360
  22.4 0.0 copy-done
  22.4 0.5 %copy.12 = f32[32]{0:T(128)} copy(f32[32]{0:T(128)S(1)} %bitcast.7) | data formatting | bytes 256
Async XLA Ops:
  20.6 1.9 %copy-start = (f32[1,32]{1,0:T(1,128)S(1)}, f32[1,32]{1,0:T(1,128)}, u32[]{:S(2)}) copy-start(f32[1,32]{1,0:T(1,128)} %get-tuple-element.5) | copy-start | bytes 388

commit v2 on v1

v2 whole, which is shorter than its diff:
```python
import functools

import jax
import jax.numpy as jnp
from jax import lax
from jax.experimental import pallas as pl
from jax.experimental.pallas import tpu as pltpu
from jax.sharding import PartitionSpec as P

LANES = 128
MESH = pl.DeviceIdType.MESH
F32 = jnp.float32
BF16 = jnp.bfloat16
NT = (((1,), (1,)), ((), ()))


def split(value, parts):
    terms = []
    for _ in range(parts):
        term = value.astype(BF16).astype(F32)
        terms.append(term)
        value = value - term
    return terms


def scatter(value_ref, var_ref, point_ref, acc, row_acc, half):
    rows = point_ref.shape[0]
    step = 8
    low_ids = lax.broadcasted_iota(jnp.int32, (half, LANES), 0)
    col_ids = lax.broadcasted_iota(jnp.int32, (2 * LANES, LANES), 0)
    slot_ids = lax.broadcasted_iota(jnp.int32, (2 * half, LANES), 0)

    def chunk(first):
        point = point_ref[pl.ds(first, step), :]
        slot = point >> 7
        upper = (slot >= half).astype(jnp.int32)
        low = slot - half * upper
        col = (point & (LANES - 1)) + LANES * upper
        y = split(value_ref[pl.ds(first, step), :], 2)
        exact = y[0] + y[1]
        raw = var_ref[pl.ds(first, step), :]
        v = split(raw, 2)
        terms = [jnp.ones_like(raw)] + y + v
        row_terms = v + split(raw * raw, 3) + split(exact * exact, 3)
        left, right, hots = [], [], []
        row_left = []
        for r in range(step):
            here = slice(r, r + 1)
            hot = (low_ids == low[here, :]).astype(F32).astype(BF16)
            blocks = []
            for term in terms:
                wide = jnp.broadcast_to(term[here, :], (16, LANES)).astype(BF16)
                blocks.append(hot * jnp.concatenate([wide] * (half // 16), 0))
            left.append(jnp.concatenate(blocks, 0))
            right.append((col_ids == col[here, :]).astype(F32).astype(BF16))
            hots.append((slot_ids == slot[here, :]).astype(F32).astype(BF16))
            row_left.append(jnp.concatenate([term[here, :] for term in row_terms], 0))
        points = lax.dot_general(
            jnp.concatenate(left, 1), jnp.concatenate(right, 1), NT, preferred_element_type=F32
        )
        by_slot = lax.dot_general(
            jnp.concatenate(row_left, 1).astype(BF16), jnp.concatenate(hots, 1), NT,
            preferred_element_type=F32,
        )
        return points, by_slot

    points, by_slot = chunk(0)
    acc[...] = points
    row_acc[...] = by_slot

    @pl.loop(1, rows // step)
    def _(i):
        points, by_slot = chunk(pl.multiple_of(i * step, step))
        acc[...] += points
        row_acc[...] += by_slot


def kernel(
    n_region, n_member, members,
    ens_hbm, value_hbm, var_hbm, point_hbm, owned_hbm, pmean_hbm, pvar_hbm,
    out_ref, post_ref,
    ens, value, var, point, owned, pmean, pvar,
    part, rs_recv, means, factors, acc, row_acc, place, place_recv,
    in_sem, rs_send, rs_got, mean_send, mean_got, f_send, f_got, pl_send, pl_got,
):
    region = lax.axis_index("region")
    me = lax.axis_index("member")
    slots = owned.shape[1]
    own = slots // n_member
    half = slots // 2
    devices = n_region * n_member
    flat = region * n_member + me

    def device(i):
        there = lax.rem(flat + i, devices)
        return there, (there // n_member, lax.rem(there, n_member))

    def peer(i):
        return {"member": lax.rem(me + i, n_member)}

    barrier = pltpu.get_barrier_semaphore()
    for i in range(1, devices):
        pl.semaphore_signal(barrier, inc=1, device_id=device(i)[1], device_id_type=MESH)
    pairs = (
        (point_hbm, point), (value_hbm, value), (var_hbm, var), (ens_hbm, ens),
        (owned_hbm, owned), (pmean_hbm, pmean), (pvar_hbm, pvar),
    )
    loads = [pltpu.make_async_copy(s, d, in_sem.at[i]) for i, (s, d) in enumerate(pairs)]
    for load in loads:
        load.start()
    for load in loads[:3]:
        load.wait()
    scatter(value, var, point, acc, row_acc, half)

    for index, (first, last) in enumerate(((0, 1), (1, 3), (3, 5))):
        both = acc[first * half : (first + 1) * half, :]
        for other in range(first + 1, last):
            both = both + acc[other * half : (other + 1) * half, :]
        table = jnp.concatenate([both[:, :LANES], both[:, LANES:]], 0)
        for k in range(n_member):
            part[k, (2 + index) * own : (3 + index) * own, :] = table[k * own : (k + 1) * own]
    sums = row_acc[...]
    rows = jnp.concatenate(
        [
            sums[0:1] + sums[1:2],
            sums[2:3] + sums[3:4] + sums[4:5],
            sums[5:6] + sums[6:7] + sums[7:8],
            jnp.zeros((5, slots), F32),
        ],
        0,
    )
    for k in range(n_member):
        part[k, 5 * own :, :] = rows

    for load in loads[3:]:
        load.wait()

    @pl.loop(0, n_member)
    def _(k):
        @pl.loop(0, own, unroll=8)
        def _(r):
            start = pl.multiple_of((k * own + r) * LANES, LANES)
            wide = ens[:, pl.ds(start, LANES)].astype(F32)
            part[k, pl.ds(r, 1), :] = jnp.sum(wide, 0, keepdims=True)
            part[k, pl.ds(own + r, 1), :] = jnp.sum(wide * wide, 0, keepdims=True)

    pl.semaphore_wait(barrier, devices - 1)
    rs = []
    for i in range(1, n_member):
        copy = pltpu.make_async_remote_copy(
            part.at[lax.rem(me + i, n_member)], rs_recv.at[i], rs_send.at[i], rs_got.at[i],
            device_id=peer(i), device_id_type=MESH,
        )
        copy.start()
        rs.append(copy)

    block = owned[...]
    groups = pmean.shape[0]
    lane_hot = (
        lax.broadcasted_iota(jnp.int32, (LANES, slots), 0) == (block & (LANES - 1))
    ).astype(F32).astype(BF16)
    table = jnp.concatenate(split(pmean[...], 3) + split(pvar[...], 3), 0).astype(BF16)
    picked = jnp.dot(table, lane_hot, preferred_element_type=F32)
    in_group = lax.broadcasted_iota(jnp.int32, (groups, slots), 0) == (block >> 7)

    def pick(first):
        total = picked[first * groups : (first + 1) * groups]
        for i in (1, 2):
            total = total + picked[(first + i) * groups : (first + i + 1) * groups]
        return jnp.sum(jnp.where(in_group, total, 0.0), 0, keepdims=True)

    prior_mean, prior_var = pick(0), pick(3)
    share = groups * LANES // devices
    lane = lax.broadcasted_iota(jnp.int32, (1, slots), 1)
    target = lax.broadcasted_iota(jnp.int32, (devices, slots), 0) == jnp.where(
        lane // own == me, block // share, -1
    )
    spots = (
        lax.broadcasted_iota(jnp.int32, (LANES, slots), 0) == lax.rem(block, share)
    ).astype(F32).astype(BF16)
    mine = lax.broadcasted_iota(jnp.int32, (own, slots), 1) == (
        lax.broadcasted_iota(jnp.int32, (own, slots), 0) + own * me
    )

    for copy in rs:
        copy.wait_recv()

    def reduced(first, last):
        total = part[me, first:last, :]
        for i in range(1, n_member):
            total = total + rs_recv[i, first:last, :]
        return total

    both = reduced(0, 2 * own)
    mean = both[:own] / members
    means[me] = mean
    ag = []
    for i in range(1, n_member):
        copy = pltpu.make_async_remote_copy(
            means.at[me], means.at[me], mean_send.at[i], mean_got.at[i],
            device_id=peer(i), device_id_type=MESH,
        )
        copy.start()
        ag.append(copy)
    spread = (both[own:] - members * mean * mean) / (members - 1)
    count = reduced(2 * own, 3 * own)
    y_sum = reduced(3 * own, 4 * own)
    v_sum = reduced(4 * own, 5 * own)
    by_slot = reduced(5 * own, 5 * own + 8)

    def to_row(table):
        column = jnp.sum(table, axis=1, keepdims=True)
        return jnp.sum(jnp.where(mine, column, 0.0), axis=0, keepdims=True)

    seen = count * spread
    so, soo = by_slot[0:1], by_slot[1:2]
    sd = by_slot[2:3] + to_row(mean * (count * mean - 2.0 * y_sum))
    sp, spp, spo = to_row(seen), to_row(seen * spread), to_row(v_sum * spread)
    weight = 2.0 * prior_mean * prior_mean * (1.0 + spp) + 4.0 * prior_mean * spo + 2.0 * soo
    post = jnp.maximum(
        (prior_mean * weight + prior_var * sp * (sd - so)) / (weight + prior_var * sp * sp), 1.0
    )

    sent = jnp.concatenate([jnp.where(target, term, 0.0) for term in split(post, 3)], 0)
    placed = lax.dot_general(sent.astype(BF16), spots, NT, preferred_element_type=F32)
    placed = placed[:devices] + placed[devices : 2 * devices] + placed[2 * devices :]
    for d in range(devices):
        place[d] = placed[d : d + 1]
    column = jnp.sum(jnp.where(mine, post, 0.0), axis=1, keepdims=True)
    factors[me] = jnp.broadcast_to(jnp.sqrt(column), (own, LANES))
    out_copies = []
    for i in range(1, devices):
        there, coords = device(i)
        copy = pltpu.make_async_remote_copy(
            place.at[there], place_recv.at[i], pl_send.at[i], pl_got.at[i],
            device_id=coords, device_id_type=MESH,
        )
        copy.start()
        out_copies.append(copy)
    for i in range(1, n_member):
        copy = pltpu.make_async_remote_copy(
            factors.at[me], factors.at[me], f_send.at[i], f_got.at[i],
            device_id=peer(i), device_id_type=MESH,
        )
        copy.start()
        ag.append(copy)
    for copy in ag:
        copy.wait_recv()

    @pl.loop(0, n_member)
    def _(k):
        @pl.loop(0, own, unroll=8)
        def _(r):
            start = pl.multiple_of((k * own + r) * LANES, LANES)
            wide = ens[:, pl.ds(start, LANES)].astype(F32)
            at = means[k, pl.ds(r, 1), :]
            out_ref[:, pl.ds(start, LANES)] = (
                at + factors[k, pl.ds(r, 1), :] * (wide - at)
            ).astype(BF16)

    for copy in out_copies:
        copy.wait_recv()
    result = place[flat]
    for i in range(1, devices):
        result = result + place_recv[i]
    post_ref[...] = result[:, :share]
    for copy in rs + ag + out_copies:
        copy.wait_send()


def body(n_region, n_member, ensemble, obs_value, obs_var, obs_point, owned, infl_mean, infl_var):
    members = ensemble.shape[0] * n_member
    slots = owned.shape[0]
    own = slots // n_member
    blocks = infl_mean.shape[0]
    devices = n_region * n_member
    share = blocks // devices
    owned = owned.reshape(1, slots)
    infl_mean = infl_mean.reshape(-1, LANES)
    infl_var = infl_var.reshape(-1, LANES)
    operands = (ensemble, obs_value, obs_var, obs_point, owned, infl_mean, infl_var)
    dma = pltpu.SemaphoreType.DMA
    inflated, post = pl.pallas_call(
        functools.partial(kernel, n_region, n_member, members),
        out_shape=(
            jax.ShapeDtypeStruct(ensemble.shape, BF16),
            jax.ShapeDtypeStruct((1, share), F32),
        ),
        in_specs=[pl.BlockSpec(memory_space=pltpu.HBM)] * len(operands),
        out_specs=(
            pl.BlockSpec(memory_space=pltpu.VMEM),
            pl.BlockSpec(memory_space=pltpu.VMEM),
        ),
        scratch_shapes=[pltpu.VMEM(a.shape, a.dtype) for a in operands]
        + [
            pltpu.VMEM((n_member, 5 * own + 8, LANES), F32),
            pltpu.VMEM((n_member, 5 * own + 8, LANES), F32),
            pltpu.VMEM((n_member, own, LANES), F32),
            pltpu.VMEM((n_member, own, LANES), F32),
            pltpu.VMEM((5 * (slots // 2), 2 * LANES), F32),
            pltpu.VMEM((8, slots), F32),
            pltpu.VMEM((devices, 1, LANES), F32),
            pltpu.VMEM((devices, 1, LANES), F32),
            dma((len(operands),)),
            dma((n_member,)), dma((n_member,)),
            dma((n_member,)), dma((n_member,)),
            dma((n_member,)), dma((n_member,)),
            dma((devices,)), dma((devices,)),
        ],
        compiler_params=pltpu.CompilerParams(collective_id=0, has_side_effects=True),
    )(*operands)
    return inflated, post.reshape(share)


def solution(mesh):
    placed = (
        P("member", "region"),
        P(("region", "member"), None),
        P(("region", "member"), None),
        P(("region", "member"), None),
        P("region"),
        P(),
        P(),
    )
    return jax.shard_map(
        functools.partial(body, mesh.shape["region"], mesh.shape["member"]),
        mesh=mesh,
        in_specs=placed,
        out_specs=(P("member", "region"), P(("region", "member"))),
        check_vma=False,
    )
```

time: 23.1 us -> 21.6 us (0.935)
  Pallas kernels: 19.9 us -> 18.3 us
    pallas_call x1, Pallas kernels: 19.9 us -> 18.3 us  [body(): pl.pallas_call(functools.partial(kernel, n_region, n_member, members), ou...]
where the time goes in v2:
time: 21.6 us; the launch traced here: 21.3 us
  Pallas kernels  18.3 us (85%)
  local copies, waits for them, and re-layouts  2.38 us (11%)
  between operations  0.65 us (3%)
    pallas_call x1, Pallas kernels, body(): pl.pallas_call(functools.partial(kernel, n_region, n_member, members), ou...  18.3 us
    unnamed x4, local copies, waits for them, and re-layouts  2.38 us

profile of v2, /device:TPU:0, one launch (start us, length us, event | category | flops | bytes accessed | tf_op | source)
XLA Modules:
  0.0 21.3 jit_solution(5741048015824838481)
XLA Ops:
  0.6 18.3 %shard_map.86 = (bf16[10,16384]{1,0:T(8,128)(2,1)}, f32[1,32]{1,0:T(1,128)}) custom-call(bf16[10,16384]{1,0:T(8,128)(2,1)} %ens_hbm.1, f32[32,128]{1,0:T(8,128)} %value_hbm.1, f32[32,128]{1,0:T(8,128)} %var_hbm.1, s32[32,128]{1,0:T(8,128)} %point_hbm.1, s32[1,128]{1,0:T(1,128)} %bitcast.6, f32[8,128]{1,0:T(8,128)} %bitcast.4, f32[8,128]{1,0:T(8,128)} %bitcast.5), custom_call_target="tpu_custom_call" | custom-call | tf_op jit(solution)/shard_map/pallas_call | solution.py:283
  18.9 0.0 copy-start
  18.9 1.9 %copy.11 = bf16[10,16384]{1,0:T(8,128)(2,1)} copy(bf16[10,16384]{1,0:T(8,128)(2,1)} %get-tuple-element.8) | data formatting | bytes 655360
  20.8 0.0 copy-done
  20.8 0.5 %copy.12 = f32[32]{0:T(128)} copy(f32[32]{0:T(128)S(1)} %bitcast.7) | data formatting | bytes 256
Async XLA Ops:
  18.9 1.9 %copy-start = (f32[1,32]{1,0:T(1,128)S(1)}, f32[1,32]{1,0:T(1,128)}, u32[]{:S(2)}) copy-start(f32[1,32]{1,0:T(1,128)} %get-tuple-element.5) | copy-start | bytes 388

commit v3 on v2

--- a/solution.py
+++ b/solution.py
@@ -23,7 +23,7 @@
     return terms
 
 
-def scatter(value_ref, var_ref, point_ref, acc, row_acc, half):
+def scatter(value_ref, var_ref, point_ref, acc, row_acc, half, first_part):
     rows = point_ref.shape[0]
     step = 8
     low_ids = lax.broadcasted_iota(jnp.int32, (half, LANES), 0)
@@ -64,15 +64,18 @@
         )
         return points, by_slot
 
-    points, by_slot = chunk(0)
-    acc[...] = points
-    row_acc[...] = by_slot
-
-    @pl.loop(1, rows // step)
-    def _(i):
+    def add(i):
         points, by_slot = chunk(pl.multiple_of(i * step, step))
         acc[...] += points
         row_acc[...] += by_slot
+
+    if first_part:
+        points, by_slot = chunk(0)
+        acc[...] = points
+        row_acc[...] = by_slot
+        pl.loop(1, rows // step // 2)(add)
+    else:
+        pl.loop(rows // step // 2, rows // step)(add)
 
 
 def kernel(
@@ -102,15 +105,43 @@
     for i in range(1, devices):
         pl.semaphore_signal(barrier, inc=1, device_id=device(i)[1], device_id_type=MESH)
     pairs = (
-        (point_hbm, point), (value_hbm, value), (var_hbm, var), (ens_hbm, ens),
+        (ens_hbm, ens), (point_hbm, point), (value_hbm, value), (var_hbm, var),
         (owned_hbm, owned), (pmean_hbm, pmean), (pvar_hbm, pvar),
     )
     loads = [pltpu.make_async_copy(s, d, in_sem.at[i]) for i, (s, d) in enumerate(pairs)]
     for load in loads:
         load.start()
-    for load in loads[:3]:
+    loads[0].wait()
+
+    @pl.loop(0, n_member)
+    def _(k):
+        @pl.loop(0, own, unroll=8)
+        def _(r):
+            start = pl.multiple_of((k * own + r) * LANES, LANES)
+            wide = ens[:, pl.ds(start, LANES)].astype(F32)
+            part[k, pl.ds(r, 1), :] = jnp.sum(wide, 0, keepdims=True)
+            part[k, pl.ds(own + r, 1), :] = jnp.sum(wide * wide, 0, keepdims=True)
+
+    for load in loads[1:]:
         load.wait()
-    scatter(value, var, point, acc, row_acc, half)
+    scatter(value, var, point, acc, row_acc, half, True)
+    pl.semaphore_wait(barrier, devices - 1)
+
+    def reduce_copies(first, count, which):
+        copies = []
+        for i in range(1, n_member):
+            copy = pltpu.make_async_remote_copy(
+                part.at[lax.rem(me + i, n_member), pl.ds(first, count), :],
+                rs_recv.at[i, pl.ds(first, count), :],
+                rs_send.at[which, i], rs_got.at[which, i],
+                device_id=peer(i), device_id_type=MESH,
+            )
+            copy.start()
+            copies.append(copy)
+        return copies
+
+    rs = reduce_copies(0, 2 * own, 0)
+    scatter(value, var, point, acc, row_acc, half, False)
 
     for index, (first, last) in enumerate(((0, 1), (1, 3), (3, 5))):
         both = acc[first * half : (first + 1) * half, :]
@@ -132,27 +163,7 @@
     for k in range(n_member):
         part[k, 5 * own :, :] = rows
 
-    for load in loads[3:]:
-        load.wait()
-
-    @pl.loop(0, n_member)
-    def _(k):
-        @pl.loop(0, own, unroll=8)
-        def _(r):
-            start = pl.multiple_of((k * own + r) * LANES, LANES)
-            wide = ens[:, pl.ds(start, LANES)].astype(F32)
-            part[k, pl.ds(r, 1), :] = jnp.sum(wide, 0, keepdims=True)
-            part[k, pl.ds(own + r, 1), :] = jnp.sum(wide * wide, 0, keepdims=True)
-
-    pl.semaphore_wait(barrier, devices - 1)
-    rs = []
-    for i in range(1, n_member):
-        copy = pltpu.make_async_remote_copy(
-            part.at[lax.rem(me + i, n_member)], rs_recv.at[i], rs_send.at[i], rs_got.at[i],
-            device_id=peer(i), device_id_type=MESH,
-        )
-        copy.start()
-        rs.append(copy)
+    rs_rest = reduce_copies(2 * own, 3 * own + 8, 1)
 
     block = owned[...]
     groups = pmean.shape[0]
@@ -203,6 +214,8 @@
         copy.start()
         ag.append(copy)
     spread = (both[own:] - members * mean * mean) / (members - 1)
+    for copy in rs_rest:
+        copy.wait_recv()
     count = reduced(2 * own, 3 * own)
     y_sum = reduced(3 * own, 4 * own)
     v_sum = reduced(4 * own, 5 * own)
@@ -264,7 +277,7 @@
     for i in range(1, devices):
         result = result + place_recv[i]
     post_ref[...] = result[:, :share]
-    for copy in rs + ag + out_copies:
+    for copy in rs + rs_rest + ag + out_copies:
         copy.wait_send()
 
 
@@ -280,6 +293,7 @@
     infl_var = infl_var.reshape(-1, LANES)
     operands = (ensemble, obs_value, obs_var, obs_point, owned, infl_mean, infl_var)
     dma = pltpu.SemaphoreType.DMA
+    operands = tuple(pltpu.with_memory_space_constraint(x, pltpu.HBM) for x in operands)
     inflated, post = pl.pallas_call(
         functools.partial(kernel, n_region, n_member, members),
         out_shape=(
@@ -302,12 +316,12 @@
             pltpu.VMEM((devices, 1, LANES), F32),
             pltpu.VMEM((devices, 1, LANES), F32),
             dma((len(operands),)),
-            dma((n_member,)), dma((n_member,)),
+            dma((2, n_member)), dma((2, n_member)),
             dma((n_member,)), dma((n_member,)),
             dma((n_member,)), dma((n_member,)),
             dma((devices,)), dma((devices,)),
         ],
-        compiler_params=pltpu.CompilerParams(collective_id=0, has_side_effects=True),
+        compiler_params=pltpu.CompilerParams(collective_id=0, has_side_effects=True, vmem_limit_bytes=12*2**20),
     )(*operands)
     return inflated, post.reshape(share)
 

time: 21.6 us -> 19.3 us (0.89)
  Pallas kernels: 18.3 us -> 17.2 us
  local copies, waits for them, and re-layouts: 2.38 us -> 1.31 us
    unnamed x4 -> x2, local copies, waits for them, and re-layouts: 2.38 us -> 1.31 us
    pallas_call x1, Pallas kernels: 18.3 us -> 17.2 us  [body(): pl.pallas_call(functools.partial(kernel, n_region, n_member, members), ou...]
where the time goes in v3:
time: 19.3 us; the launch traced here: 19.2 us
  Pallas kernels  17.2 us (89%)
  local copies, waits for them, and re-layouts  1.31 us (7%)
  between operations  0.64 us (3%)
    pallas_call x1, Pallas kernels, body(): pl.pallas_call(functools.partial(kernel, n_region, n_member, members), ou...  17.2 us
    unnamed x2, local copies, waits for them, and re-layouts  1.31 us

profile of v3, /device:TPU:0, one launch (start us, length us, event | category | flops | bytes accessed | tf_op | source)
XLA Modules:
  0.0 19.2 jit_solution(4723080301852422217)
XLA Ops:
  0.6 17.2 %shard_map.86 = (bf16[10,16384]{1,0:T(8,128)(2,1)S(1)}, f32[1,32]{1,0:T(1,128)S(1)}) custom-call(bf16[10,16384]{1,0:T(8,128)(2,1)} %ens_hbm.1, f32[32,128]{1,0:T(8,128)} %value_hbm.1, f32[32,128]{1,0:T(8,128)} %var_hbm.1, s32[32,128]{1,0:T(8,128)} %point_hbm.1, s32[1,128]{1,0:T(1,128)} %bitcast.7, f32[8,128]{1,0:T(8,128)} %bitcast.5, f32[8,128]{1,0:T(8,128)} %bitcast.6), custom_call_target="tpu_custom_call" | custom-call | tf_op jit(solution)/shard_map/pallas_call | solution.py:297
  17.9 0.8 %copy.11 = bf16[10,16384]{1,0:T(8,128)(2,1)} copy(bf16[10,16384]{1,0:T(8,128)(2,1)S(1)} %get-tuple-element.8) | data formatting | bytes 655360
  18.7 0.5 %copy.12 = f32[32]{0:T(128)} copy(f32[32]{0:T(128)S(1)} %bitcast.4) | data formatting | bytes 256
